TPU v7x, 256 devices: a whole 4x4x8 slice. The times are simulated.
256 devices in a mesh: row: 16 (over x, z_hi), col: 8 (over y, core), ga: 2 (over z_lo).
Axes of the slice: x: 4, y: 4, z: 8 (z_hi: 4, z_lo: 2; z = z_hi * 2 + z_lo), core: 2. Of those that a mesh axis runs over, the one named last changes fastest.
Arguments:
- pair_density: float32 [512, 24, 3072], P('row', None, 'ga'), may hold values from -6 to 6
- coulomb: float32 [3072], P('ga'), may hold values from 0.1 to 2
Outputs:
- kernel: float32 [12288, 12288], P('row', 'col')
All inputs are finite; a program needn't handle non-finite values.
Results may differ from a plain program's by a relative error of at most 0.00011.
Values sent between devices are 32-bit elements; how exact they have to be, the bound alone decides.
A program may use at most 64 MiB of HBM per device.

v0:
```python
import jax
import jax.numpy as jnp
from jax import lax
from jax.sharding import PartitionSpec as P


def rows_for(lines, peers):
    spare = -lines.shape[0] % peers
    if not spare:
        return lines
    return jnp.concatenate([lines, jnp.zeros((spare, *lines.shape[1:]), lines.dtype)])


def from_root(value, axis, root):
    lines = jnp.where(lax.axis_index(axis) == root, value, jnp.zeros_like(value)).reshape(
        -1, *value.shape[1:][-1:]
    )
    padded = rows_for(lines, lax.axis_size(axis))
    own = lax.psum_scatter(padded, axis, scatter_dimension=0, tiled=True)
    return lax.all_gather(own, axis, axis=0, tiled=True)[: len(lines)].reshape(value.shape)


def sent_to_all(value, axis):
    copies = jnp.broadcast_to(value, (lax.axis_size(axis), *value.shape))
    return lax.all_to_all(copies, axis, split_axis=0, concat_axis=0, tiled=True)


def taken_together(value, axis):
    return sent_to_all(value, axis).sum(axis=0)


def contract(left_rows, right_rows):
    return lax.dot_general(
        left_rows,
        right_rows,
        (((1,), (1,)), ((), ())),
        precision=lax.Precision.HIGHEST,
        preferred_element_type=jnp.float32,
    )


def local(pair_density, coulomb):
    row_count = lax.axis_size("row")
    col_count = lax.axis_size("col")
    here_row = lax.axis_index("row")
    here_col = lax.axis_index("col")
    doubled = 2.0 * coulomb
    local_k, bands, g_width = pair_density.shape
    grouped = pair_density.reshape(local_k // col_count, col_count, bands, g_width)
    own_columns = lax.dynamic_index_in_dim(grouped, here_col, 1, keepdims=False)
    columns = lax.all_gather(own_columns, "row", axis=0, tiled=True)
    ratio = row_count // col_count
    chosen = lax.dynamic_index_in_dim(
        columns.reshape(local_k, ratio, bands, g_width), here_row // col_count, 1, keepdims=False
    )
    rows_data = from_root(chosen, "col", here_row % col_count)
    weighted = rows_data.reshape(local_k * bands, g_width) * doubled[None, :]
    partial_value = contract(weighted, columns.reshape(columns.shape[0] * bands, g_width))
    summed = taken_together(partial_value, "ga")
    total_k = local_k * row_count
    return summed / jnp.float32(total_k)


def solution(mesh):
    placed = (P("row", None, "ga"), P("ga"))
    return jax.shard_map(
        local, mesh=mesh, in_specs=placed, out_specs=P("row", "col"), check_vma=False
    )
```

profile of v0, /device:TPU:1, one launch (start us, length us, event | category | flops | bytes accessed | tf_op | source)
XLA Modules:
  0.0 380.6 jit_solution(15559402277794939784)
XLA Ops:
  6.5 0.0 all-gather.6.cloned.1.call-start
  6.5 1.9 constant_dynamic-slice_fusion
  8.5 0.0 all-gather.6.cloned.1.call-update
  8.5 0.0 reduce-scatter.2.cloned.1.call-start
  8.6 125.7 %all-gather.6.cloned.1.call-done = f32[64,1,24,1536]{3,2,1,0:T(8,128)} async-done(((f32[4,1,24,1536]{3,2,1,0:T(8,128)}), f32[64,1,24,1536]{3,2,1,0:T(8,128)}) %all-gather.6.cloned.1.call-update) | async-done | bytes 9437200 | tf_op jit(solution)/shard_map/all_gather | solution.py:51
  134.3 5.0 %dynamic-slice_select_fusion = f32[32,1,24,1536]{3,2,1,0:T(8,128)} fusion(f32[32,2,24,1536]{3,2,1,0:T(8,128)} %bitcast.6, s32[]{:T(128)S(6)} %select_n.35, pred[]{:T(512)S(6)} %eq.5), kind=kLoop, calls=%fused_computation.2 | loop fusion | flops 1179648 | bytes 9437189 | tf_op jit(solution)/shard_map/jit(_where)/select_n | solution.py:15
  139.3 0.0 copy-start
  139.3 0.0 reduce-scatter.2.cloned.1.call-update
  139.3 0.0 all-gather.4.cloned.1.call-start
  139.3 44.3 %reduce-scatter.2.cloned.1.call-done = f32[96,1536]{1,0:T(8,128)} async-done(((f32[768,1536]{1,0:T(8,128)}), f32[96,1536]{1,0:T(8,128)}) %reduce-scatter.2.cloned.1.call-update) | async-done | bytes 589840 | tf_op jit(solution)/shard_map/reduce_scatter | solution.py:19
  183.7 0.0 all-gather.4.cloned.1.call-update
  183.7 0.0 copy-done
  183.7 40.9 %all-gather.4.cloned.1.call-done = f32[768,1536]{1,0:T(8,128)} async-done(((f32[96,1536]{1,0:T(8,128)}), f32[768,1536]{1,0:T(8,128)}) %all-gather.4.cloned.1.call-update) | async-done | bytes 4718608 | tf_op jit(solution)/shard_map/all_gather | solution.py:20
  224.7 28.0 %fusion = f32[768,1536]{1,0:T(8,128)S(1)} fusion(f32[1536,1536]{1,0:T(8,128)} %bitcast.7, f32[768,1536]{1,0:T(8,128)} %all-gather.4.cloned.1.call-done, f32[1536]{0:T(1024)S(1)} %broadcast_multiply_fusion.1), kind=kOutput, calls=%fused_computation | convolution fusion | flops 21744451584 | bytes 18880512 | tf_op jit(solution)/shard_map/dot_general | solution.py:33
  252.7 1.2 broadcast_in_dim.8
  253.9 107.9 %all_to_all.5 = f32[2,768,1536]{2,1,0:T(8,128)} all-to-all(f32[2,768,1536]{2,1,0:T(8,128)S(1)} %broadcast_in_dim.8), channel_id=1, replica_groups=mesh['row'=16,'col'=8,'ga'=2] {'ga'}, dimensions={0} | all-to-all | bytes 18874368 | tf_op jit(solution)/shard_map/all_to_all | solution.py:25
  361.8 7.3 %reduce_sum.9 = f32[768,1536]{1,0:T(8,128)} reduce(f32[2,768,1536]{2,1,0:T(8,128)} %all_to_all.5, f32[]{:T(128)} %constant.51.clone.1), dimensions={0}, to_apply=%region_1.2 | reduce | flops 1179648 | bytes 14155780 | tf_op jit(solution)/shard_map/reduce_sum | solution.py:29
  369.1 5.0 %broadcast_multiply_fusion = f32[768,1536]{1,0:T(8,128)} fusion(f32[768,1536]{1,0:T(8,128)} %reduce_sum.9), kind=kLoop, calls=%fused_computation.3 | loop fusion | flops 1179648 | bytes 9437184 | tf_op jit(solution)/shard_map/div | solution.py:61
  (1 shorter events, 0.0 us)
Async XLA Ops:
  6.5 127.7 %all-gather.6.cloned.1.call-start = ((), (), s32[]{:S(2)}) async-start(), calls=%async_computation.4 | async-start | bytes 10027008 | tf_op jit(solution)/shard_map/all_gather | solution.py:51
  8.5 175.2 %reduce-scatter.2.cloned.1.call-start = ((), (), s32[]{:S(2)}) async-start(), calls=%async_computation.2 | async-start | bytes 5308416 | tf_op jit(solution)/shard_map/reduce_scatter | solution.py:19
  139.3 44.4 %copy-start = (f32[1536]{0:T(1024)S(1)}, f32[1536]{0:T(1024)}, u32[]{:S(2)}) copy-start(f32[1536]{0:T(1024)} %param.3) | copy-start | bytes 18436
  139.3 85.4 %all-gather.4.cloned.1.call-start = ((), (), s32[]{:S(2)}) async-start(), calls=%async_computation.3 | async-start | bytes 5308416 | tf_op jit(solution)/shard_map/all_gather | solution.py:20
Sparse Core Ops, SparseCore 0:
  9.8 124.4 all-gather.5
  139.4 44.2 reduce-scatter.1
  185.5 39.1 all-gather.3
where the time goes:
time: 381 us
  waiting for transfers between devices  211 us (55%)
  blocking collectives  108 us (28%)
  matrix products  28 us (7%)
  other arithmetic  17.3 us (5%)
  between operations  13.2 us (3%)
    all_gather x1, waiting for transfers between devices, local(): columns = lax.all_gather(own_columns, 'row', axis=0, tiled=True)  126 us
    all_to_all x1, blocking collectives, sent_to_all(): return lax.all_to_all(copies, axis, split_axis=0, concat_axis=0, tiled=True)  108 us
    reduce_scatter x1, waiting for transfers between devices, from_root(): own = lax.psum_scatter(padded, axis, scatter_dimension=0, tiled=True)  44.3 us
    all_gather x1, waiting for transfers between devices, from_root(): lax.all_gather(own, axis, axis=0, tiled=True)[:len(lines)]  40.9 us
    dot_general x1, matrix products, contract(): lax.dot_general(left_rows, right_rows, (((1,), (1,)), ((), ())), precisio...  28 us
  transfers between devices with their start and end apart: 3, of which 3 were waited for; matrix products, arithmetic and copies ran while one was open for 0% of the time, Pallas kernels for 0%

commit v1 on v0

--- a/solution.py
+++ b/solution.py
@@ -48,7 +48,9 @@
     local_k, bands, g_width = pair_density.shape
     grouped = pair_density.reshape(local_k // col_count, col_count, bands, g_width)
     own_columns = lax.dynamic_index_in_dim(grouped, here_col, 1, keepdims=False)
-    columns = lax.all_gather(own_columns, "row", axis=0, tiled=True)
+    columns = jnp.concatenate(
+        lax.all_to_all(jnp.stack([own_columns] * lax.axis_size("row")), "row", 0, 0), axis=0
+    )
     ratio = row_count // col_count
     chosen = lax.dynamic_index_in_dim(
         columns.reshape(local_k, ratio, bands, g_width), here_row // col_count, 1, keepdims=False

time: 381 us -> 487 us (1.28)
  waiting for transfers between devices: 211 us -> 301 us
  starting transfers between devices: 0.09 us -> 11.7 us
    all_to_all x0 -> x1, waiting for transfers between devices: none -> 212 us  [local(): lax.all_to_all(jnp.stack([own_columns] * lax.axis_size('row')), 'row', 0, 0)]
    all_gather x1 -> x0, waiting for transfers between devices: 126 us -> none  [local(): columns = lax.all_gather(own_columns, 'row', axis=0, tiled=True)]
    all_to_all x0 -> x1, starting transfers between devices: none -> 11.6 us  [local(): lax.all_to_all(jnp.stack([own_columns] * lax.axis_size('row')), 'row', 0, 0)]
    another operation x0 -> x2, local copies, waits for them, and re-layouts: none -> 5.96 us  [local(): jnp.stack([own_columns] * lax.axis_size('row'))]
where the time goes in v1:
time: 487 us
  waiting for transfers between devices  301 us (62%)
  blocking collectives  108 us (22%)
  matrix products  28 us (6%)
  other arithmetic  17.3 us (4%)
  between operations  13.5 us (3%)
  starting transfers between devices  11.7 us (2%)
  local copies, waits for them, and re-layouts  7.19 us (1%)
    all_to_all x1, waiting for transfers between devices, local(): lax.all_to_all(jnp.stack([own_columns] * lax.axis_size('row')), 'row', 0, 0)  212 us
    all_to_all x1, blocking collectives, sent_to_all(): return lax.all_to_all(copies, axis, split_axis=0, concat_axis=0, tiled=True)  108 us
    reduce_scatter x1, waiting for transfers between devices, from_root(): own = lax.psum_scatter(padded, axis, scatter_dimension=0, tiled=True)  48.5 us
    all_gather x1, waiting for transfers between devices, from_root(): lax.all_gather(own, axis, axis=0, tiled=True)[:len(lines)]  40.9 us
    dot_general x1, matrix products, contract(): lax.dot_general(left_rows, right_rows, (((1,), (1,)), ((), ())), precisio...  28 us
    all_to_all x1, starting transfers between devices, local(): lax.all_to_all(jnp.stack([own_columns] * lax.axis_size('row')), 'row', 0, 0)  11.6 us
  transfers between devices with their start and end apart: 3, of which 3 were waited for; matrix products, arithmetic and copies ran while one was open for 0% of the time, Pallas kernels for 0%

profile of v1, /device:TPU:1, one launch (start us, length us, event | category | flops | bytes accessed | tf_op | source)
XLA Modules:
  0.0 486.7 jit_solution(8287528157460049204)
XLA Ops:
  6.5 1.1 dynamic-slice_bitcast_fusion
  7.6 4.9 stack.5
  12.5 11.6 %all-to-all-start = ((f32[16,4,24,1536]{3,2,1,0:T(8,128)}), f32[16,4,24,1536]{3,2,1,0:T(8,128)}, u32[]{:S(2)}, u32[]{:S(2)}) async-start(f32[16,4,24,1536]{3,2,1,0:T(8,128)} %stack.5), calls=%async_computation | async-start | bytes 18874368 | tf_op jit(solution)/shard_map/all_to_all | solution.py:52
  24.1 0.0 reduce-scatter.2.cloned.1.call-start
  24.2 211.7 %all-to-all-done = f32[16,4,24,1536]{3,2,1,0:T(8,128)} async-done(((f32[16,4,24,1536]{3,2,1,0:T(8,128)}), f32[16,4,24,1536]{3,2,1,0:T(8,128)}, u32[]{:S(2)}, u32[]{:S(2)}) %all-to-all-start) | async-done | bytes 9437216 | tf_op jit(solution)/shard_map/all_to_all | solution.py:52
  235.9 5.0 %dynamic-slice_select_fusion = f32[32,1,24,1536]{3,2,1,0:T(8,128)} fusion(f32[32,2,24,1536]{3,2,1,0:T(8,128)} %bitcast.2, s32[]{:T(128)S(6)} %select_n.35, pred[]{:T(512)S(6)} %eq.5), kind=kLoop, calls=%fused_computation.2 | loop fusion | flops 1179648 | bytes 9437189 | tf_op jit(solution)/shard_map/jit(_where)/select_n | solution.py:15
  240.9 0.0 copy-start
  240.9 0.0 reduce-scatter.2.cloned.1.call-update
  240.9 0.0 all-gather.2.cloned.1.call-start
  240.9 48.5 %reduce-scatter.2.cloned.1.call-done = f32[96,1536]{1,0:T(8,128)} async-done(((f32[768,1536]{1,0:T(8,128)}), f32[96,1536]{1,0:T(8,128)}) %reduce-scatter.2.cloned.1.call-update) | async-done | bytes 589840 | tf_op jit(solution)/shard_map/reduce_scatter | solution.py:19
  289.5 0.0 all-gather.2.cloned.1.call-update
  289.5 0.0 copy-done
  289.5 40.9 %all-gather.2.cloned.1.call-done = f32[768,1536]{1,0:T(8,128)} async-done(((f32[96,1536]{1,0:T(8,128)}), f32[768,1536]{1,0:T(8,128)}) %all-gather.2.cloned.1.call-update) | async-done | bytes 4718608 | tf_op jit(solution)/shard_map/all_gather | solution.py:20
  330.4 28.0 %fusion = f32[768,1536]{1,0:T(8,128)S(1)} fusion(f32[1536,1536]{1,0:T(8,128)} %bitcast.4, f32[768,1536]{1,0:T(8,128)} %all-gather.2.cloned.1.call-done, f32[1536]{0:T(1024)S(1)} %broadcast_multiply_fusion.1), kind=kOutput, calls=%fused_computation | convolution fusion | flops 21744451584 | bytes 18880512 | tf_op jit(solution)/shard_map/dot_general | solution.py:33
  358.5 1.2 broadcast_in_dim.8
  359.7 107.9 %all_to_all.10 = f32[2,768,1536]{2,1,0:T(8,128)} all-to-all(f32[2,768,1536]{2,1,0:T(8,128)S(1)} %broadcast_in_dim.8), channel_id=1, replica_groups=mesh['row'=16,'col'=8,'ga'=2] {'ga'}, dimensions={0} | all-to-all | bytes 18874368 | tf_op jit(solution)/shard_map/all_to_all | solution.py:25
  467.5 7.3 %reduce_sum.9 = f32[768,1536]{1,0:T(8,128)} reduce(f32[2,768,1536]{2,1,0:T(8,128)} %all_to_all.10, f32[]{:T(128)} %constant.51.clone.1), dimensions={0}, to_apply=%region_1.2 | reduce | flops 1179648 | bytes 14155780 | tf_op jit(solution)/shard_map/reduce_sum | solution.py:29
  474.8 5.0 %broadcast_multiply_fusion = f32[768,1536]{1,0:T(8,128)} fusion(f32[768,1536]{1,0:T(8,128)} %reduce_sum.9), kind=kLoop, calls=%fused_computation.3 | loop fusion | flops 1179648 | bytes 9437184 | tf_op jit(solution)/shard_map/div | solution.py:63
  (1 shorter events, 0.0 us)
Async XLA Ops:
  12.5 223.4 %all-to-all-start = ((f32[16,4,24,1536]{3,2,1,0:T(8,128)}), f32[16,4,24,1536]{3,2,1,0:T(8,128)}, u32[]{:S(2)}, u32[]{:S(2)}) async-start(f32[16,4,24,1536]{3,2,1,0:T(8,128)} %stack.5), calls=%async_computation | async-start | bytes 18874368 | tf_op jit(solution)/shard_map/all_to_all | solution.py:52
  24.1 265.4 %reduce-scatter.2.cloned.1.call-start = ((), (), s32[]{:S(2)}) async-start(), calls=%async_computation.3 | async-start | bytes 5308416 | tf_op jit(solution)/shard_map/reduce_scatter | solution.py:19
  240.9 48.6 %copy-start = (f32[1536]{0:T(1024)S(1)}, f32[1536]{0:T(1024)}, u32[]{:S(2)}) copy-start(f32[1536]{0:T(1024)} %param.3) | copy-start | bytes 18436
  240.9 89.5 %all-gather.2.cloned.1.call-start = ((), (), s32[]{:S(2)}) async-start(), calls=%async_computation.4 | async-start | bytes 5308416 | tf_op jit(solution)/shard_map/all_gather | solution.py:20
Sparse Core Ops, SparseCore 0:
  241.0 48.4 reduce-scatter.1
  291.3 39.0 all-gather.1
